TPU v7x, 32 devices: a whole 2x2x4 slice. The times are simulated.
32 devices in a mesh: chan: 4 (over x, core), bl: 8 (over z, y).
Axes of the slice: x: 2, y: 2, z: 4, core: 2. Of those that a mesh axis runs over, the one named last changes fastest.
Arguments:
- vis_value: bfloat16 [4, 8, 2, 2048], P('chan', 'bl'), may hold values from -6 to 6
- vis_weight: bfloat16 [4, 8, 2048], P('chan', 'bl'), may hold values from 0.19921875 to 5
- kernel: bfloat16 [4, 8, 64, 2048], P('chan', 'bl'), may hold values from 0.049804688 to 1
- tile_index: int32 [4, 8, 2048], P('chan', 'bl'), may hold values from 0 to 262143
- plane_index: int32 [4, 8, 2048], P('chan', 'bl'), may hold values from 0 to 7
- chan_index: int32 [4, 8, 2048], P('chan', 'bl'), may hold values from 0 to 15
- chan_offset: float32 [4, 16], P('chan'), may hold values from -0.4 to 0.4
- counts: int32 [4, 8], P('chan', 'bl'), may hold values from 256 to 2048, as said below
Outputs:
- taylor_coeffs: float32 [3, 32768], P(None, ('chan', 'bl'))
Inputs may be any that keep to these rules, and one draw needn't show every extreme that they name: `counts`: each device's number of live visibility slots; slots from that number on are ignored. In every draw some device has exactly 2048.
All inputs are finite; a program needn't handle non-finite values.
Results may differ from a plain program's by a relative error of at most 0.0003.
Values may be sent and summed in bfloat16 or wider, within the bound.
A program may use at most 128 MiB of HBM per device.

v0:
```python
import jax
import jax.numpy as jnp
from jax import lax
from jax.sharding import PartitionSpec as P

NPIX = 4096
TILE = 8
TAYLOR = 3
MOMENTS = 5
WPLANES = 8
STRIP = 8
BLK = 256


two_pi = 6.283185307179586
w_step = 40.0
inner_radix = 128
highest = lax.Precision.HIGHEST


def block_terms(values, weights, kernel, tiles, planes, chans, offsets, live_mask):
    block_size = weights.shape[0]
    ntiles = NPIX // TILE
    channel_ids = jnp.arange(offsets.shape[0], dtype=jnp.int32)
    taylor_coord = jnp.sum(
        jnp.where(chans[:, None] == channel_ids[None, :], offsets[None, :], 0.0), axis=1
    )
    live_weight = jnp.where(live_mask, weights.astype(jnp.float32), 0.0)
    kernel_taps = kernel.astype(jnp.float32).reshape(TILE, TILE, block_size)
    strip_rows = jnp.arange(STRIP, dtype=jnp.int32) - STRIP // 2
    grid_cols = (
        (tiles // ntiles)[None, :] * TILE + jnp.arange(TILE, dtype=jnp.int32)[:, None] - NPIX // 2
    )
    phase_index = grid_cols[:, None, :] * strip_rows[None, :, None] % NPIX
    phase_angle = phase_index.astype(jnp.float32) * (two_pi / NPIX)
    cosine = jnp.cos(phase_angle)
    sine = jnp.sin(phase_angle)
    tile_real = jnp.sum(kernel_taps[:, :, None, :] * cosine[:, None, :, :], axis=0)
    tile_imag = jnp.sum(kernel_taps[:, :, None, :] * sine[:, None, :, :], axis=0)
    base_real = live_weight * values[0].astype(jnp.float32)
    base_imag = live_weight * values[1].astype(jnp.float32)
    power_list = [jnp.ones_like(taylor_coord)]
    for power_id in range(MOMENTS - 1):
        power_list.append(power_list[power_id] * taylor_coord)
    power_stack = jnp.stack(power_list[:TAYLOR], axis=0)
    coeff_real = (base_real[None, :] * power_stack)[None, :, None, :]
    coeff_imag = (base_imag[None, :] * power_stack)[None, :, None, :]
    part_real = coeff_real * tile_real[:, None] - coeff_imag * tile_imag[:, None]
    part_imag = coeff_real * tile_imag[:, None] + coeff_imag * tile_real[:, None]
    columns = TILE * TAYLOR * STRIP
    updates = jnp.stack(
        [part_real.reshape(columns, block_size), part_imag.reshape(columns, block_size)]
    )
    updates = jnp.transpose(updates, (0, 2, 1))
    target_rows = planes * ntiles + tiles % ntiles
    tap_sums = jnp.sum(kernel_taps, axis=(0, 1))
    weighted_taps = live_weight * tap_sums
    moment_add = jnp.stack(
        [jnp.sum(weighted_taps * power_list[moment_id]) for moment_id in range(MOMENTS)]
    )
    return (updates, target_rows, moment_add)


def grid_slots(arrays, low_limit, high_limit, offsets):
    slot_count = arrays[1].shape[0]
    middle = slot_count // 2
    ntiles = NPIX // TILE
    low_blocks = (jnp.minimum(low_limit, middle) + BLK - 1) // BLK
    high_blocks = (jnp.maximum(high_limit - middle, 0) + BLK - 1) // BLK

    def one_block(block_turn, state_pair):
        uv_grid, moments = state_pair
        block_id = jnp.where(
            block_turn < low_blocks, block_turn, middle // BLK + block_turn - low_blocks
        )
        first_slot = block_id * BLK
        slot_limit = jnp.where(first_slot < middle, low_limit, high_limit)
        live_mask = first_slot + jnp.arange(BLK, dtype=jnp.int32) < slot_limit
        pieces = [
            lax.dynamic_slice_in_dim(source, first_slot, BLK, source.ndim - 1) for source in arrays
        ]
        updates, target_rows, moment_add = block_terms(
            pieces[0], pieces[1], pieces[2], pieces[3], pieces[4], pieces[5], offsets, live_mask
        )
        return (uv_grid.at[:, target_rows].add(updates), moments + moment_add)

    initial = (
        jnp.zeros((2, WPLANES * ntiles, TILE * TAYLOR * STRIP), jnp.float32),
        jnp.zeros((MOMENTS,), jnp.float32),
    )
    return lax.fori_loop(0, low_blocks + high_blocks, one_block, initial)


def complex_table(cosine, sine):
    return jnp.stack(
        [jnp.stack([cosine, -sine], axis=0), jnp.stack([sine, cosine], axis=0)], axis=0
    )


def screen_grid(plane_ids, column_grid):
    cell_size = 0.5 / NPIX
    strip_rows = jnp.arange(STRIP, dtype=jnp.int32) - STRIP // 2
    xcoord = strip_rows.astype(jnp.float32) * cell_size
    ycoord = (column_grid - NPIX // 2).astype(jnp.float32) * cell_size
    radius = xcoord[:, None, None] * xcoord[:, None, None] + ycoord[None] * ycoord[None]
    lowered = -radius / (1.0 + jnp.sqrt(1.0 - radius))
    w_value = w_step * (plane_ids.astype(jnp.float32) - 0.5 * (WPLANES - 1))
    return two_pi * w_value[:, None, None, None] * lowered[None]


def strip_image(uv_grid):
    ntiles = NPIX // TILE
    outer = NPIX // inner_radix
    sub_tiles = inner_radix // TILE
    width = TAYLOR * STRIP
    plane_count = uv_grid.shape[1] // ntiles
    cube = uv_grid.reshape(2, plane_count, outer, sub_tiles, TILE, width)
    cube = jnp.transpose(cube, (0, 1, 5, 2, 3, 4)).reshape(
        2, plane_count, width, outer, inner_radix
    )
    outer_ids = jnp.arange(outer, dtype=jnp.int32)
    inner_ids = jnp.arange(inner_radix, dtype=jnp.int32)
    angle_outer = (outer_ids[:, None] * outer_ids[None, :] % outer).astype(jnp.float32) * (
        two_pi / outer
    )
    table_outer = complex_table(jnp.cos(angle_outer), jnp.sin(angle_outer))
    section_one = jnp.einsum("oiav,ipRvn->opRan", table_outer, cube, precision=highest)
    twist_angle = (outer_ids[:, None] * inner_ids[None, :] % NPIX).astype(jnp.float32) * (
        two_pi / NPIX
    )
    twist_sign = 1.0 - 2.0 * (inner_ids % 2).astype(jnp.float32)
    twist_real = jnp.cos(twist_angle) * twist_sign
    twist_imag = jnp.sin(twist_angle) * twist_sign
    twisted = jnp.stack(
        [
            section_one[0] * twist_real - section_one[1] * twist_imag,
            section_one[0] * twist_imag + section_one[1] * twist_real,
        ]
    )
    angle_inner = (inner_ids[:, None] * inner_ids[None, :] % inner_radix).astype(jnp.float32) * (
        two_pi / inner_radix
    )
    table_inner = complex_table(jnp.cos(angle_inner), jnp.sin(angle_inner))
    section_two = jnp.einsum("oicn,ipRan->opRac", table_inner, twisted, precision=highest)
    column_grid = inner_ids[None, :] * outer + outer_ids[:, None]
    parity = 1.0 - 2.0 * (column_grid % 2).astype(jnp.float32)
    angles = screen_grid(jnp.arange(plane_count, dtype=jnp.int32), column_grid)
    spectra = section_two.reshape(2, plane_count, TAYLOR, STRIP, outer, inner_radix)
    image = jnp.sum(
        parity * (jnp.cos(angles)[:, None] * spectra[0] - jnp.sin(angles)[:, None] * spectra[1]),
        axis=0,
    )
    return jnp.transpose(image, (0, 1, 3, 2)).reshape(TAYLOR, STRIP * NPIX)


def solve_taylor(moments, images):
    entry_00, entry_01, entry_02 = (moments[0], moments[1], moments[2])
    entry_11, entry_12, entry_22 = (moments[2], moments[3], moments[4])
    minor_00 = entry_11 * entry_22 - entry_12 * entry_12
    minor_01 = entry_02 * entry_12 - entry_01 * entry_22
    minor_02 = entry_01 * entry_12 - entry_02 * entry_11
    minor_11 = entry_00 * entry_22 - entry_02 * entry_02
    minor_12 = entry_01 * entry_02 - entry_00 * entry_12
    minor_22 = entry_00 * entry_11 - entry_01 * entry_01
    determinant = entry_00 * minor_00 + entry_01 * minor_01 + entry_02 * minor_02
    first = (minor_00 * images[0] + minor_01 * images[1] + minor_02 * images[2]) / determinant
    second = (minor_01 * images[0] + minor_11 * images[1] + minor_12 * images[2]) / determinant
    third = (minor_02 * images[0] + minor_12 * images[1] + minor_22 * images[2]) / determinant
    return jnp.stack([first, second, third])


def body(vis_value, vis_weight, kernel, tile_index, plane_index, chan_index, chan_offset, counts):
    own_arrays = (
        vis_value[0, 0],
        vis_weight[0, 0],
        kernel[0, 0],
        tile_index[0, 0],
        plane_index[0, 0],
        chan_index[0, 0],
    )
    own_count = counts[0, 0]
    offsets = chan_offset[0]
    uv_grid, moments = grid_slots(own_arrays, own_count, own_count, offsets)
    moments_total = lax.psum(moments, ("chan", "bl"))
    image = strip_image(uv_grid)
    group_share = lax.psum_scatter(image, "chan", scatter_dimension=1, tiled=True)
    image_share = lax.psum_scatter(group_share, "bl", scatter_dimension=1, tiled=True)
    return solve_taylor(moments_total, image_share)


def solution(mesh):
    in_specs = (
        P("chan", "bl", None, None),
        P("chan", "bl", None),
        P("chan", "bl", None, None),
        P("chan", "bl", None),
        P("chan", "bl", None),
        P("chan", "bl", None),
        P("chan", None),
        P("chan", "bl"),
    )
    out_specs = P(None, ("chan", "bl"))
    return jax.shard_map(body, mesh=mesh, in_specs=in_specs, out_specs=out_specs, check_vma=False)
```

profile of v0, /device:TPU:0, one launch (start us, length us, event | category | flops | bytes accessed | tf_op | source)
XLA Modules:
  0.0 648.0 jit_solution(10190639277119250371)
XLA Ops:
  8.0 0.7 reduce.2
  8.8 5.4 broadcast_in_dim.59
  14.2 177.6 %while.15 = (s32[]{:T(128)}, f32[2,4096,192]{2,0,1:T(2,128)}, f32[5]{0:T(128)S(1)}, s32[]{:T(128)}, s32[]{:T(128)}, /*index=5*/s32[2048]{0:T(1024)}, s32[2048]{0...) while((s32[]{:T(128)}, f32[2,4096,192]{2,0,1:T(2,128)}, ...), condition=%wide.region_11.12_spmd, body=%wide.region_0.11_spmd.sunk | while | flops 1292563 | bytes 3926113 | solution.py:91
  14.2 0.8 fusion.76
  15.3 0.8 convert_bitcast_fusion.2
  16.2 0.8 dynamic-slice_convert_fusion.3
  17.0 0.8 convert_reduce_fusion.2
  17.8 0.7 fusion.78
  18.5 0.8 dynamic_slice.69
  19.8 26.2 %scatter_fusion = f32[2,4096,192]{2,0,1:T(2,128)} fusion(f32[2,4096,192]{2,0,1:T(2,128)} %get-tuple-element.438, s32[256]{0:T(256)S(1)} %get-tuple-element.396, f32[256,2,192]{2,1,0:T(2,128)S(1)} %copy.44), kind=kCustom, calls=%fused_computation.clone.1 | custom fusion | flops 98304 | bytes 1180672 | tf_op jit(solution)/shard_map/while/body/scatter-add | solution.py:85
  46.0 0.7 fusion.80
  46.6 3.1 stack.120
  49.8 0.8 fusion.76
  50.9 0.8 convert_bitcast_fusion.2
  51.8 0.8 dynamic-slice_convert_fusion.3
  52.6 0.8 convert_reduce_fusion.2
  53.4 0.7 fusion.78
  54.1 0.8 dynamic_slice.69
  55.4 26.2 %scatter_fusion = f32[2,4096,192]{2,0,1:T(2,128)} fusion(f32[2,4096,192]{2,0,1:T(2,128)} %get-tuple-element.438, s32[256]{0:T(256)S(1)} %get-tuple-element.396, f32[256,2,192]{2,1,0:T(2,128)S(1)} %copy.44), kind=kCustom, calls=%fused_computation.clone.1 | custom fusion | flops 98304 | bytes 1180672 | tf_op jit(solution)/shard_map/while/body/scatter-add | solution.py:85
  81.5 0.7 fusion.80
  82.2 3.1 stack.120
  85.3 0.8 fusion.76
  86.5 0.8 convert_bitcast_fusion.2
  87.3 0.8 dynamic-slice_convert_fusion.3
  88.2 0.8 convert_reduce_fusion.2
  88.9 0.7 fusion.78
  89.7 0.8 dynamic_slice.69
  90.9 26.1 %scatter_fusion = f32[2,4096,192]{2,0,1:T(2,128)} fusion(f32[2,4096,192]{2,0,1:T(2,128)} %get-tuple-element.438, s32[256]{0:T(256)S(1)} %get-tuple-element.396, f32[256,2,192]{2,1,0:T(2,128)S(1)} %copy.44), kind=kCustom, calls=%fused_computation.clone.1 | custom fusion | flops 98304 | bytes 1180672 | tf_op jit(solution)/shard_map/while/body/scatter-add | solution.py:85
  117.0 0.7 fusion.80
  117.7 3.1 stack.120
  120.9 0.8 fusion.76
  122.0 0.8 convert_bitcast_fusion.2
  122.9 0.8 dynamic-slice_convert_fusion.3
  123.7 0.8 convert_reduce_fusion.2
  124.5 0.7 fusion.78
  125.2 0.8 dynamic_slice.69
  126.5 26.0 %scatter_fusion = f32[2,4096,192]{2,0,1:T(2,128)} fusion(f32[2,4096,192]{2,0,1:T(2,128)} %get-tuple-element.438, s32[256]{0:T(256)S(1)} %get-tuple-element.396, f32[256,2,192]{2,1,0:T(2,128)S(1)} %copy.44), kind=kCustom, calls=%fused_computation.clone.1 | custom fusion | flops 98304 | bytes 1180672 | tf_op jit(solution)/shard_map/while/body/scatter-add | solution.py:85
  152.4 0.7 fusion.80
  153.1 3.1 stack.120
  156.2 0.8 fusion.76
  157.4 0.8 convert_bitcast_fusion.2
  158.2 0.8 dynamic-slice_convert_fusion.3
  159.1 0.8 convert_reduce_fusion.2
  159.8 0.7 fusion.78
  160.6 0.8 dynamic_slice.69
  161.8 26.0 %scatter_fusion = f32[2,4096,192]{2,0,1:T(2,128)} fusion(f32[2,4096,192]{2,0,1:T(2,128)} %get-tuple-element.438, s32[256]{0:T(256)S(1)} %get-tuple-element.396, f32[256,2,192]{2,1,0:T(2,128)S(1)} %copy.44), kind=kCustom, calls=%fused_computation.clone.1 | custom fusion | flops 98304 | bytes 1180672 | tf_op jit(solution)/shard_map/while/body/scatter-add | solution.py:85
  187.8 0.7 fusion.80
  188.5 3.1 stack.120
  191.8 7.2 %copy.20 = f32[2,4096,192]{2,1,0:T(8,128)} copy(f32[2,4096,192]{2,0,1:T(2,128)} %get-tuple-element.222) | data formatting | bytes 12582912 | tf_op jit(solution)/shard_map/while | solution.py:91
  199.0 21.8 %reshape.607 = f32[2,8,32,16,8,24]{5,4,3,2,1,0:T(8,128)} reshape(f32[2,4096,192]{2,1,0:T(8,128)} %copy.20) | data formatting | bytes 12582912 | tf_op jit(solution)/shard_map/reshape | solution.py:117
  220.8 36.3 %copy.24 = f32[2,8,24,32,128,1]{3,4,0,5,2,1:T(8,128)} copy(f32[2,8,24,32,128,1]{2,4,3,1,0,5:T(8,128)} %bitcast.111) | data formatting | bytes 12582912 | tf_op jit(solution)/shard_map/reshape | solution.py:118
  257.4 3.7 multiply_cosine_fusion
  261.1 28.6 %convolution_bitcast_fusion = f32[2,8,24,32,128]{4,3,0,2,1:T(8,128)S(1)} fusion(f32[2,8,24,32,128,1]{3,4,0,5,2,1:T(8,128)} %copy.24, f32[1,2,32,32]{3,2,1,0:T(8,128)S(1)} %get-tuple-element.279, f32[1,2,32,32]{3,2,1,0:T(8,128)S(1)} %get-tuple-element.278), kind=kOutput, calls=%fused_computation.62 | convolution fusion | flops 1207963648 | bytes 12599296 | tf_op jit(solution)/shard_map/oiav,ipRvn->opRan/dot_general | solution.py:127
  289.7 0.9 multiply_subtract_fusion.1
  290.7 5.1 fusion.24
  296.2 0.4 mul.896
  296.6 1.6 fusion.23
  298.2 13.7 %copy.38 = f32[3,8,128,32]{0,3,2,1:T(8,128)} copy(f32[3,8,128,32]{2,3,1,0:T(8,128)S(1)} %bitcast.118) | data formatting | bytes 786432
  312.0 232.8 %reduce-scatter.7.cloned.1.call-done = f32[8192,3]{1,0:T(8,128)} async-done(((f32[32768,3]{1,0:T(8,128)}), f32[8192,3]{1,0:T(8,128)}) %reduce-scatter.7.cloned.1.call-update) | async-done | bytes 98320
  544.8 41.9 %psum.7 = f32[5]{0:T(128)S(1)} all-reduce(f32[5]{0:T(128)S(1)} %get-tuple-element.221), channel_id=1, replica_groups=mesh['chan'=4,'bl'=8] {'chan','bl'}, use_global_device_ids=true, to_apply=%region_12.13 | all-reduce | flops 5 | bytes 40 | tf_op jit(solution)/shard_map/psum | solution.py:184
  586.7 0.7 fusion.69
  602.9 35.3 %reduce-scatter.9.cloned.1.call-done = f32[1024,3]{1,0:T(8,128)} async-done(((f32[8192,3]{1,0:T(8,128)}), f32[1024,3]{1,0:T(8,128)}) %reduce-scatter.9.cloned.1.call-update) | async-done | bytes 12304
  638.2 1.7 fusion.68
  640.6 0.6 pad_maximum_fusion.1
  (85 shorter events, 6.6 us)
Async XLA Ops:
  6.5 538.2 %reduce-scatter.7.cloned.1.call-start = ((), (), s32[]{:S(2)}) async-start(), calls=%async_computation.2 | async-start | bytes 20971520
  8.8 5.4 copy-start
  311.9 326.3 %reduce-scatter.9.cloned.1.call-start = ((), (), s32[]{:S(2)}) async-start(), calls=%async_computation.3 | async-start | bytes 4718592
Sparse Core Ops, SparseCore 0:
  312.0 232.6 reduce-scatter.6
  548.4 89.7 reduce-scatter.8
where the time goes:
time: 655 us; the launch traced here: 648 us
  waiting for transfers between devices  268 us (41%)
  other arithmetic  165 us (25%)
  local copies, waits for them, and re-layouts  109 us (17%)
  blocking collectives  41.9 us (6%)
  matrix products  33.7 us (5%)
  between operations  29.8 us (5%)
    unnamed x4, waiting for transfers between devices  268 us
    scatter-add x5, other arithmetic, one_block(): return (uv_grid.at[:, target_rows].add(updates), moments + moment_add)  130 us
    psum x1, blocking collectives, body(): moments_total = lax.psum(moments, ('chan', 'bl'))  41.9 us
    reshape x1, local copies, waits for them, and re-layouts, strip_image(): jnp.transpose(cube, (0, 1, 5, 2, 3, 4))  36.3 us
    dot_general x1, matrix products, strip_image(): jnp.einsum('oiav,ipRvn->opRan', table_outer, cube, precision=highest)  28.6 us
    reshape x1, local copies, waits for them, and re-layouts, strip_image(): cube = uv_grid.reshape(2, plane_count, outer, sub_tiles, TILE, width)  21.8 us
    another operation x5, local copies, waits for them, and re-layouts, block_terms(): jnp.stack([jnp.sum(weighted_taps * power_list[moment_id]) for moment_id i...  15.6 us
    unnamed x6, local copies, waits for them, and re-layouts  14.3 us
  transfers between devices with their start and end apart: 2, of which 2 were waited for; matrix products, arithmetic and copies ran while one was open for 0% of the time, Pallas kernels for 0%

commit v1 on v0

v1 whole, which is shorter than its diff:
```python
import functools

import numpy as np
import jax
import jax.numpy as jnp
from jax import lax
from jax.experimental import pallas as pl
from jax.experimental.pallas import tpu as pltpu
from jax.sharding import PartitionSpec as P

NPIX = 4096
TILE = 8
TAYLOR = 3
MOMENTS = 5
WPLANES = 8
STRIP = 8
BLK = 256
LANES = 128

two_pi = 2.0 * np.pi
w_step = 40.0
ntiles = NPIX // TILE
radix = 256
fine = NPIX // radix
half = fine * STRIP
MESH = pl.DeviceIdType.MESH


def split(x):
    high = x.astype(jnp.bfloat16)
    low = (x - high.astype(jnp.float32)).astype(jnp.bfloat16)
    return high, low


@functools.cache
def tables():
    f32 = np.float32
    bf16 = jnp.bfloat16

    def two(x):
        x = x.astype(f32)
        high = x.astype(bf16)
        return high, (x - high.astype(f32)).astype(bf16)

    rows = np.arange(STRIP) - STRIP // 2
    taps = np.zeros((2, TILE, STRIP, TILE, TILE))
    angle = two_pi * np.arange(TILE)[:, None] * rows[None, :] / NPIX
    for e in range(TILE):
        taps[0, e, :, :, e] = np.cos(angle).T
        taps[1, e, :, :, e] = np.sin(angle).T
    tap_high, tap_low = two(taps.reshape(2 * TILE * STRIP, TILE * TILE))
    tap_table = np.concatenate([tap_high, tap_low], axis=1)
    ids = np.arange(radix)
    angle = two_pi * (ids[:, None] * ids[None, :] % radix) / radix
    coarse_high, coarse_low = two(np.concatenate([np.cos(angle), np.sin(angle)], axis=1))
    coarse = np.concatenate([coarse_high, coarse_low], axis=0)
    cells = np.arange(fine)
    angle = two_pi * cells[:, None] * ids[None, :] / NPIX
    sign = 1.0 - 2.0 * ((cells[:, None] + ids[None, :]) % 2)
    twist = np.stack([np.cos(angle) * sign, np.sin(angle) * sign])
    twist = np.repeat(twist, STRIP, axis=1).astype(f32)
    angle = two_pi * (cells[:, None] * cells[None, :] % fine) / fine
    eye = np.eye(STRIP)
    cosine = np.einsum("me,lL->lmeL", np.cos(angle), eye).reshape(half, half)
    sine = np.einsum("me,lL->lmeL", np.sin(angle), eye).reshape(half, half)
    fine_high, fine_low = two(np.block([[cosine, -sine], [sine, cosine]]))
    fine_table = np.concatenate([fine_high, fine_low, fine_high], axis=1)
    cell_size = 0.5 / NPIX
    x = rows * cell_size
    y = (np.arange(NPIX) - NPIX // 2) * cell_size
    radius = x[:, None] ** 2 + y[None, :] ** 2
    lowered = -radius / (1.0 + np.sqrt(1.0 - radius))
    w = w_step * (np.arange(WPLANES // 2) - 0.5 * (WPLANES - 1))
    angle = two_pi * w[:, None, None] * lowered[None]
    angle = angle.reshape(WPLANES // 2, STRIP * fine, radix)
    screen = np.stack([np.cos(angle), np.sin(angle)], axis=1).astype(f32)
    return tap_table, coarse, twist, fine_table, screen


def image_kernel(
    count_ref, offset_ref, value_ref, weight_ref, kernel_ref, tile_ref, plane_ref, chan_ref,
    tap_ref, coarse_hbm, twist_hbm, fine_hbm, screen_hbm,
    image_ref, moment_ref, coarse_ref, twist_ref, fine_ref, screen_ref, grid_ref, upd_ref, mom_ref, turn_ref, flat_ref, sems,
):
    loads = [
        pltpu.make_async_copy(source, target, sems.at[i])
        for i, (source, target) in enumerate((
            (coarse_hbm, coarse_ref), (twist_hbm, twist_ref),
            (fine_hbm, fine_ref), (screen_hbm, screen_ref),
        ))
    ]
    for load in loads:
        load.start()
    count = count_ref[0, 0]
    grid_ref[...] = jnp.zeros_like(grid_ref)
    mom_ref[...] = jnp.zeros_like(mom_ref)

    def one_block(block, carry):
        first = pl.multiple_of(block * BLK, BLK)
        here = pl.ds(first, BLK)
        slot = first + lax.broadcasted_iota(jnp.int32, (1, BLK), 1)
        tiles = tile_ref[:, here]
        planes = plane_ref[:, here]
        chans = chan_ref[:, here]
        coord = jnp.zeros((1, BLK), jnp.float32)
        for c in range(offset_ref.shape[1]):
            coord = jnp.where(chans == c, offset_ref[0, c], coord)
        weight = weight_ref[0:1, here].astype(jnp.float32)
        weight = jnp.where(slot < count, weight, 0.0)
        taps = kernel_ref[:, here]
        value = value_ref[:, here].astype(jnp.float32)
        base_real = weight * value[0:1]
        base_imag = weight * value[1:2]

        u_tile = lax.shift_right_logical(tiles, 9)
        v_tile = tiles & (ntiles - 1)
        strip = lax.broadcasted_iota(jnp.int32, (STRIP, BLK), 0) - STRIP // 2
        phase = ((u_tile - ntiles // 2) * strip) & (ntiles - 1)
        angle = phase.astype(jnp.float32) * (two_pi / ntiles)
        cosine = jnp.cos(angle)
        sine = jnp.sin(angle)
        z_real = base_real * cosine - base_imag * sine
        z_imag = base_real * sine + base_imag * cosine

        sums = jnp.dot(
            tap_ref[...], jnp.concatenate([taps, taps], axis=0),
            preferred_element_type=jnp.float32,
        )
        sum_real = sums[: TILE * STRIP].reshape(TILE, STRIP, BLK)
        sum_imag = sums[TILE * STRIP :].reshape(TILE, STRIP, BLK)
        part_real = (sum_real * z_real[None] - sum_imag * z_imag[None]).reshape(-1, BLK)
        part_imag = (sum_real * z_imag[None] + sum_imag * z_real[None]).reshape(-1, BLK)
        odd = (v_tile & 1).astype(jnp.float32)
        even = 1.0 - odd
        for k in range(TAYLOR):
            for c, part in enumerate((part_real, part_imag)):
                for side, mask in enumerate((even, odd)):
                    high, low = split(part * mask)
                    row = (k * 2 + c) * half + side * (half // 2)
                    upd_ref[row : row + half // 2, :BLK] = high
                    upd_ref[row : row + half // 2, BLK:] = low
            if k + 1 < TAYLOR:
                part_real = part_real * coord
                part_imag = part_imag * coord

        weighted = weight * jnp.sum(taps.astype(jnp.float32), axis=0, keepdims=True)
        for m in range(MOMENTS):
            mom_ref[m : m + 1, :] += weighted
            weighted = weighted * coord

        target = planes * radix + lax.shift_right_logical(v_tile, 1)
        column = jnp.transpose(jnp.broadcast_to(target.astype(jnp.float32), (LANES, BLK)))
        column = jnp.concatenate([column, column], axis=1)
        update = upd_ref[...]
        lane = lax.broadcasted_iota(jnp.int32, (BLK, radix), 1).astype(jnp.float32)
        for p in range(WPLANES):
            hot = jnp.where(column == lane + float(p * radix), 1.0, 0.0).astype(jnp.bfloat16)
            grid_ref[p] += jnp.dot(
                update, jnp.concatenate([hot, hot], axis=0),
                preferred_element_type=jnp.float32,
            )
        return carry

    lax.fori_loop(0, (count + BLK - 1) // BLK, one_block, 0)
    moment_ref[...] = jnp.broadcast_to(
        jnp.sum(mom_ref[...], axis=1, keepdims=True), moment_ref.shape
    )

    for load in loads:
        load.wait()
    coarse_high = coarse_ref[:radix]
    coarse_table = jnp.concatenate([coarse_high, coarse_ref[radix:], coarse_high], axis=0)
    turn_ref[...] = jnp.zeros_like(turn_ref)

    def one_plane(p, carry):
        high, low = split(grid_ref[p])
        spectra = jnp.dot(
            jnp.concatenate([high, high, low], axis=1), coarse_table,
            preferred_element_type=jnp.float32,
        )
        mirror = jnp.minimum(p, WPLANES - 1 - p)
        sign = jnp.where(p < WPLANES // 2, 1.0, -1.0)
        screen_real = screen_ref[mirror, 0]
        screen_imag = screen_ref[mirror, 1] * sign
        for k in range(TAYLOR):
            real = spectra[2 * k * half : (2 * k + 1) * half]
            imag = spectra[(2 * k + 1) * half : (2 * k + 2) * half]
            f_real = real[:, :radix] - imag[:, radix:]
            f_imag = imag[:, :radix] + real[:, radix:]
            x_real = f_real * twist_ref[0] - f_imag * twist_ref[1]
            x_imag = f_real * twist_ref[1] + f_imag * twist_ref[0]
            x_high, x_low = split(jnp.concatenate([x_real, x_imag], axis=0))
            y = jnp.dot(
                fine_ref[...], jnp.concatenate([x_high, x_high, x_low], axis=0),
                preferred_element_type=jnp.float32,
            )
            turn_ref[k] += y[:half] * screen_real - y[half:] * screen_imag
        return carry

    lax.fori_loop(0, WPLANES, one_plane, 0)
    pieces = radix // LANES
    chunks, _, rows, _ = image_ref.shape
    for k in range(TAYLOR):
        for h in range(pieces):
            flat_ref[pl.ds(h, half, stride=pieces), :] = turn_ref[k, :, h * LANES : (h + 1) * LANES]
        image_ref[:, k] = flat_ref[...].reshape(chunks, rows, LANES)


def local_image(chunks, count, offsets, value, weight, kernel, tiles, planes, chans):
    rows = STRIP * NPIX // (chunks * LANES)
    consts = [jnp.asarray(t) for t in tables()]
    smem = pl.BlockSpec(memory_space=pltpu.SMEM)
    vmem = pl.BlockSpec(memory_space=pltpu.VMEM)
    hbm = pl.BlockSpec(memory_space=pl.ANY)
    columns = 2 * TAYLOR * half
    return pl.pallas_call(
        image_kernel,
        out_shape=(
            jax.ShapeDtypeStruct((chunks, TAYLOR, rows, LANES), jnp.float32),
            jax.ShapeDtypeStruct((8, LANES), jnp.float32),
        ),
        in_specs=[smem, smem] + [vmem] * 7 + [hbm] * 4,
        out_specs=(vmem, vmem),
        scratch_shapes=[pltpu.VMEM(c.shape, c.dtype) for c in consts[1:]]
        + [
            pltpu.VMEM((WPLANES, columns, radix), jnp.float32),
            pltpu.VMEM((columns, 2 * BLK), jnp.bfloat16),
            pltpu.VMEM((8, BLK), jnp.float32),
            pltpu.VMEM((TAYLOR, half, radix), jnp.float32),
            pltpu.VMEM((half * radix // LANES, LANES), jnp.float32),
            pltpu.SemaphoreType.DMA((4,)),
        ],
        compiler_params=pltpu.CompilerParams(vmem_limit_bytes=56 * 1024 * 1024),
        name="local_image",
    )(count, offsets, value, weight, kernel, tiles, planes, chans, *consts)


def solve_taylor(moments, images):
    entry_00, entry_01, entry_02 = (moments[0], moments[1], moments[2])
    entry_11, entry_12, entry_22 = (moments[2], moments[3], moments[4])
    minor_00 = entry_11 * entry_22 - entry_12 * entry_12
    minor_01 = entry_02 * entry_12 - entry_01 * entry_22
    minor_02 = entry_01 * entry_12 - entry_02 * entry_11
    minor_11 = entry_00 * entry_22 - entry_02 * entry_02
    minor_12 = entry_01 * entry_02 - entry_00 * entry_12
    minor_22 = entry_00 * entry_11 - entry_01 * entry_01
    determinant = entry_00 * minor_00 + entry_01 * minor_01 + entry_02 * minor_02
    first = (minor_00 * images[0] + minor_01 * images[1] + minor_02 * images[2]) / determinant
    second = (minor_01 * images[0] + minor_11 * images[1] + minor_12 * images[2]) / determinant
    third = (minor_02 * images[0] + minor_12 * images[1] + minor_22 * images[2]) / determinant
    return first, second, third


def reduce_kernel(
    n_chan, n_bl, image_ref, moment_ref, out_ref,
    work_ref, land_ref, sum_ref, mom_send_ref, mom_land_ref, bl_land_ref, bl_mom_ref,
    send_sem, recv_sem, mom_send_sem, mom_recv_sem, bl_send, bl_recv, blm_send, blm_recv,
):
    chan = lax.axis_index("chan")
    bl = lax.axis_index("bl")
    steps = n_chan.bit_length() - 1

    def partner(s):
        return chan + (1 - 2 * ((chan // 2**s) % 2)) * 2**s

    def peer(d):
        return lax.rem(bl + d, n_bl)

    barrier = pltpu.get_barrier_semaphore()
    for s in range(steps):
        pl.semaphore_signal(barrier, inc=1, device_id=(partner(s), bl), device_id_type=MESH)
    for d in range(1, n_bl):
        pl.semaphore_signal(barrier, inc=1, device_id=(chan, peer(d)), device_id_type=MESH)
    pl.semaphore_wait(barrier, steps + n_bl - 1)

    slot = 0
    for s in range(steps):
        stride = 2 ** (s + 1)
        pieces = n_chan // stride
        copies = [
            pltpu.make_async_remote_copy(
                src_ref=moment_ref if s == 0 else mom_send_ref.at[s],
                dst_ref=mom_land_ref.at[s],
                send_sem=mom_send_sem.at[s], recv_sem=mom_recv_sem.at[s],
                device_id=(partner(s), bl), device_id_type=MESH,
            )
        ]
        for i in range(pieces):
            if s == 0:
                source = image_ref.at[partner(0) % 2 + i * 2]
            else:
                source = work_ref.at[s - 1, (partner(s) // 2**s) % 2 + 2 * i]
            copies.append(
                pltpu.make_async_remote_copy(
                    src_ref=source, dst_ref=land_ref.at[slot + i],
                    send_sem=send_sem.at[slot + i], recv_sem=recv_sem.at[slot + i],
                    device_id=(partner(s), bl), device_id_type=MESH,
                )
            )
        for copy in copies:
            copy.start()
        copies[0].wait()
        before = moment_ref[...] if s == 0 else mom_send_ref[s]
        mom_send_ref[s + 1] = before + mom_land_ref[s]
        for i in range(pieces):
            copies[1 + i].wait()
            if s == 0:
                own = image_ref[chan % 2 + i * 2]
            else:
                own = work_ref[s - 1, (chan // 2**s) % 2 + 2 * i]
            if s + 1 < steps:
                work_ref[s, i] = own + land_ref[slot + i]
            else:
                sum_ref[...] = own + land_ref[slot + i]
        slot += pieces

    copies = []
    for d in range(1, n_bl):
        copies.append(
            pltpu.make_async_remote_copy(
                src_ref=mom_send_ref.at[steps], dst_ref=bl_mom_ref.at[d],
                send_sem=blm_send.at[d], recv_sem=blm_recv.at[d],
                device_id=(chan, peer(d)), device_id_type=MESH,
            )
        )
        copies.append(
            pltpu.make_async_remote_copy(
                src_ref=sum_ref.at[peer(d)], dst_ref=bl_land_ref.at[d],
                send_sem=bl_send.at[d], recv_sem=bl_recv.at[d],
                device_id=(chan, peer(d)), device_id_type=MESH,
            )
        )
    for copy in copies:
        copy.start()
    moments = mom_send_ref[steps]
    images = sum_ref[bl]
    for d in range(1, n_bl):
        copies[2 * d - 2].wait()
        copies[2 * d - 1].wait()
        moments = moments + bl_mom_ref[d]
        images = images + bl_land_ref[d]
    solved = solve_taylor([moments[m : m + 1] for m in range(MOMENTS)], images)
    for k in range(TAYLOR):
        out_ref[k] = solved[k]


def reduce_solve(n_chan, n_bl, image, moment):
    chunks, taylor, rows, lanes = image.shape
    image = image.reshape(n_chan, n_bl, taylor, rows, lanes)
    vmem = pl.BlockSpec(memory_space=pltpu.VMEM)
    block = (n_bl, taylor, rows, lanes)
    steps = n_chan.bit_length() - 1
    dma = pltpu.SemaphoreType.DMA
    return pl.pallas_call(
        functools.partial(reduce_kernel, n_chan, n_bl),
        out_shape=jax.ShapeDtypeStruct((taylor, rows, lanes), jnp.float32),
        in_specs=[vmem, vmem],
        out_specs=vmem,
        scratch_shapes=[
            pltpu.VMEM((max(steps - 1, 1), n_chan // 2) + block, jnp.float32),
            pltpu.VMEM((n_chan - 1,) + block, jnp.float32),
            pltpu.VMEM(block, jnp.float32),
            pltpu.VMEM((steps + 1, 8, lanes), jnp.float32),
            pltpu.VMEM((steps, 8, lanes), jnp.float32),
            pltpu.VMEM((n_bl, taylor, rows, lanes), jnp.float32),
            pltpu.VMEM((n_bl, 8, lanes), jnp.float32),
            dma((n_chan - 1,)), dma((n_chan - 1,)), dma((steps,)), dma((steps,)),
            dma((n_bl,)), dma((n_bl,)), dma((n_bl,)), dma((n_bl,)),
        ],
        compiler_params=pltpu.CompilerParams(collective_id=0, has_side_effects=True),
        name="reduce_solve",
    )(image, moment)


def solution(mesh):
    n_chan = mesh.shape["chan"]
    n_bl = mesh.shape["bl"]

    def body(vis_value, vis_weight, kernel, tile_index, plane_index, chan_index, chan_offset, counts):
        image, moment = local_image(
            n_chan * n_bl, counts, chan_offset, vis_value[0, 0], vis_weight[0], kernel[0, 0],
            tile_index[0], plane_index[0], chan_index[0],
        )
        out = reduce_solve(n_chan, n_bl, image, moment)
        return out.reshape(TAYLOR, -1)

    in_specs = (
        P("chan", "bl", None, None),
        P("chan", "bl", None),
        P("chan", "bl", None, None),
        P("chan", "bl", None),
        P("chan", "bl", None),
        P("chan", "bl", None),
        P("chan", None),
        P("chan", "bl"),
    )
    out_specs = P(None, ("chan", "bl"))
    return jax.shard_map(body, mesh=mesh, in_specs=in_specs, out_specs=out_specs, check_vma=False)
```

time: 655 us -> 51.7 us (0.08); the launches traced: 648 us -> 52.3 us
  waiting for transfers between devices: 268 us -> 0 us
  other arithmetic: 165 us -> 0 us
  local copies, waits for them, and re-layouts: 109 us -> 1.32 us
  Pallas kernels: 0 us -> 50.3 us
  blocking collectives: 41.9 us -> 0 us
  matrix products: 33.7 us -> 0 us
  between operations: 29.8 us -> 0.67 us
    unnamed x4 -> x0, waiting for transfers between devices: 268 us -> none
    scatter-add x5 -> x0, other arithmetic: 130 us -> none  [one_block(): return (uv_grid.at[:, target_rows].add(updates), moments + moment_add)]
    reshape x2 -> x0, local copies, waits for them, and re-layouts: 58.1 us -> none  [the longest x1 36.3 us: strip_image(): jnp.transpose(cube, (0, 1, 5, 2, 3, 4))]
    pallas_call x0 -> x2, Pallas kernels: none -> 50.3 us  [the longest x1 26.7 us: local_image(): pl.pallas_call(image_kernel, out_shape=(jax.ShapeDtypeStruct((chunks, TAY...]
    psum x1 -> x0, blocking collectives: 41.9 us -> none  [body(): moments_total = lax.psum(moments, ('chan', 'bl'))]
    dot_general x2 -> x0, matrix products: 33.7 us -> none  [the longest x1 28.6 us: strip_image(): jnp.einsum('oiav,ipRvn->opRan', table_outer, cube, precision=highest)]
    another operation x11 -> x0, local copies, waits for them, and re-layouts: 15.6 us -> none  [the longest x5 15.6 us: block_terms(): jnp.stack([jnp.sum(weighted_taps * power_list[moment_id]) for moment_id i...]
    unnamed x6 -> x1, local copies, waits for them, and re-layouts: 14.3 us -> 1.32 us
  transfers between devices with their start and end apart: 2 -> 0, of which waited for: 2 -> 0; matrix products, arithmetic and copies ran while one was open for 0% -> 0% of each run, Pallas kernels for 0% -> 0%
where the time goes in v1:
time: 51.7 us; the launch traced here: 52.3 us
  Pallas kernels  50.3 us (97%)
  local copies, waits for them, and re-layouts  1.32 us (3%)
  between operations  0.67 us (1%)
    pallas_call x1, Pallas kernels, local_image(): pl.pallas_call(image_kernel, out_shape=(jax.ShapeDtypeStruct((chunks, TAY...  26.7 us
    pallas_call x1, Pallas kernels, reduce_solve(): pl.pallas_call(functools.partial(reduce_kernel, n_chan, n_bl), out_shape=...  23.6 us
    unnamed x1, local copies, waits for them, and re-layouts  1.32 us

profile of v1, /device:TPU:0, one launch (start us, length us, event | category | flops | bytes accessed | tf_op | source)
XLA Modules:
  0.0 52.3 jit_solution(15127628166221393265)
XLA Ops:
  0.7 26.7 %local_image.1 = (f32[32,3,8,128]{3,2,1,0:T(8,128)}, f32[8,128]{1,0:T(8,128)}) custom-call(s32[1,1]{1,0:T(1,128)S(6)} %copy.17.count_ref, f32[1,16]{1,0:T(1,128)} %offset_ref.1, bf16[2,2048]{1,0:T(2,128)(2,1)} %bitcast.14, bf16[1,2048]{1,0:T(2,128)(2,1)} %bitcast.15, bf16[64,2048]{1,0:T(8,128)(2,1)} %bitcast.12, s32[1,2048]{1,0:T(1,128)} %bitcast.16, ...), custom_call_target="tpu_custom_call" | custom-call | tf_op jit(solution)/shard_map/local_image/pallas_call | solution.py:216
  27.4 23.6 %reduce_solve.1 = f32[3,8,128]{2,1,0:T(8,128)} custom-call(f32[4,8,3,8,128]{4,3,2,1,0:T(8,128)} %bitcast.11, f32[8,128]{1,0:T(8,128)} %get-tuple-element.8.moment_ref), custom_call_target="tpu_custom_call" | custom-call | tf_op jit(solution)/shard_map/reduce_solve/pallas_call | solution.py:354
  51.0 1.3 %copy.16 = f32[1,3,8,128]{3,1,2,0:T(4,128)} copy(f32[1,3,8,128]{3,2,1,0:T(8,128)} %bitcast.13) | data formatting | bytes 24576
